TPU v7x, 32 devices: a whole 2x2x4 slice. The times are simulated.
32 devices in a mesh: row: 4 (over y, x), col: 8 (over z, core).
Axes of the slice: x: 2, y: 2, z: 4, core: 2. Of those that a mesh axis runs over, the one named last changes fastest.
Arguments:
- depth: float32 [256, 4096], P('row', 'col'), may hold values from 0 to 1
- rainfall: float32 [256, 4096], P('row', 'col'), may hold values from 0.05 to 0.5
- conveyance: float32 [256, 4096], P('row', 'col'), may hold values from 0.2 to 5
- flow_dir: int32 [256, 4096], P('row', 'col'), may hold values from 0 to 7, as said below
- outlet: int32 [256, 4096], P('row', 'col'), may hold values 0 or 1
Outputs:
- new_depth: float32 [256, 4096], P('row', 'col')
- discharge: float32 [256, 4096], P('row', 'col')
Inputs may be any that keep to these rules, and one draw needn't show every extreme that they name: `flow_dir`: each cell's code is 0 to 7.
All inputs are finite; a program needn't handle non-finite values. No bound on the sum of `outlet` on one device may be relied on, other than what follows from the above.
Results may differ from a plain program's by a relative error of at most 0.00002.
Values sent between devices are 32-bit elements; how exact they have to be, the bound alone decides.
A program may use at most 64 MiB of HBM per device.

v0:
```python
import functools

import jax
import jax.numpy as jnp
from jax import lax
from jax.experimental import pallas as pl
from jax.experimental.pallas import tpu as pltpu
from jax.sharding import PartitionSpec as P

SUBSTEPS = 3
PASSES = 64
OFFSETS = ((0, 1), (1, 1), (1, 0), (1, -1), (0, -1), (-1, -1), (-1, 0), (-1, 1))
LANES = 128
SUB = 8
NEAR = 8
MARGIN = 32
GROUPS = PASSES // MARGIN
SPARE = 0
MESH = pl.DeviceIdType.MESH


def kernel(
    row_peers, col_peers,
    depth_ref, rain_ref, conv_ref, dir_ref, outlet_ref,
    level_ref, discharge_ref,
    depth_ext, rain_ext, coef_ext, route_ext, far_ext, acc_ext, plain, pack_out, pack_in,
    acc, rain, coef, level, share, masks,
    send_sem, recv_sem,
):
    rows, cols = depth_ref.shape
    total = depth_ext.shape[1]
    bands = total // SUB
    wide = cols + LANES
    own = cols // LANES
    my_row, my_col = lax.axis_index("row"), lax.axis_index("col")

    def exists(dr, dc):
        r, c = my_row + dr, my_col + dc
        ok = None
        for test in ((r >= 0, r < row_peers) if dr else ()) + ((c >= 0, c < col_peers) if dc else ()):
            ok = test if ok is None else jnp.logical_and(ok, test)
        return ok

    def row_place(dr, width):
        if dr == 0:
            return (pl.ds(0, rows), pl.ds(0, rows))
        if dr < 0:
            return (pl.ds(0, width), pl.ds(rows, width))
        return (pl.ds(rows - width, width), pl.ds(total - width, width))

    def col_place(dc):
        if dc == 0:
            return (pl.ds(0, own), pl.ds(0, own))
        if dc < 0:
            return (pl.ds(0, 1), pl.ds(own, 1))
        return (pl.ds(own - 1, 1), pl.ds(own + 1, 1))

    def copy(slot, k, src, dst, width):
        dr, dc = OFFSETS[k]
        (rs, rd), (cs, cd) = row_place(dr, width), col_place(dc)
        return pltpu.make_async_remote_copy(
            src_ref=src.at[cs, rs],
            dst_ref=dst.at[cd, rd],
            send_sem=send_sem.at[slot, k],
            recv_sem=recv_sem.at[slot, k],
            device_id=(my_row + dr, my_col + dc),
            device_id_type=MESH,
        )

    every = (1, 3, 5, 7, 2, 6, 0, 4)
    slanted = (1, 3, 5, 7, 2, 6)
    straight, corners = (2, 6, 0, 4), (1, 3, 5, 7)

    def send(slot, src, dst, width, order=every):
        for k in order:
            @pl.when(exists(*OFFSETS[k]))
            def _(k=k):
                copy(slot, k, src, dst, width).start()

    def receive(slot, src, dst, width, order=every):
        for k in order:
            dr, dc = OFFSETS[k]
            there = exists(-dr, -dc)

            @pl.when(there)
            def _(k=k):
                copy(slot, k, src, dst, width).wait_recv()

            @pl.when(jnp.logical_not(there))
            def _(dr=dr, dc=dc):
                _, rd = row_place(dr, width)
                _, cd = col_place(dc)
                dst[cd, rd] = jnp.zeros((cd.size, rd.size, LANES), dst.dtype)

    def sent_out(slot, src, dst, width, order=every):
        for k in order:
            @pl.when(exists(*OFFSETS[k]))
            def _(k=k):
                copy(slot, k, src, dst, width).wait_send()

    barrier = pltpu.get_barrier_semaphore()
    for dr, dc in OFFSETS:
        @pl.when(exists(dr, dc))
        def _(dr=dr, dc=dc):
            pl.semaphore_signal(
                barrier, inc=1, device_id=(my_row + dr, my_col + dc), device_id_type=MESH
            )
    for c in range(own):
        at = pl.ds(c * LANES, LANES)
        mine = pl.ds(0, rows)
        depth_ext[c, mine] = depth_ref[:, at]
        rain_ext[c, mine] = rain_ref[:, at]
        code = dir_ref[:, at]
        route = jnp.where(outlet_ref[:, at] == 1, 0, code + 1)
        route_ext[c, mine] = route
        far_ext[c, mine] = route
        coef_ext[c, mine] = conv_ref[:, at] * jnp.where(
            (code & 1) == 1, jnp.float32(0.70710678), jnp.float32(1.0)
        )
    def reach(index, peers):
        return 1 + jnp.where(index > 0, 1, 0) + jnp.where(index < peers - 1, 1, 0)

    pl.semaphore_wait(barrier, reach(my_row, row_peers) * reach(my_col, col_peers) - 1)

    firsts = (depth_ext, coef_ext, rain_ext, route_ext)
    far_slot, level_slot = (len(firsts), len(firsts) + 1)
    for slot, ext in enumerate(firsts):
        send(slot, ext, ext, NEAR)
    send(far_slot, far_ext, far_ext, MARGIN, slanted)
    unused = pl.ds(rows + NEAR, total - rows - 2 * NEAR)
    for ext in firsts:
        ext[:, unused] = jnp.zeros((own + 2, total - rows - 2 * NEAR, LANES), ext.dtype)
    if SPARE:
        for ext in (far_ext,) + tuple(acc_ext.at[g] for g in range(GROUPS)):
            ext[:, pl.ds(rows + MARGIN, SPARE)] = jnp.zeros((own + 2, SPARE, LANES), ext.dtype)
    for slot, ext in enumerate(firsts):
        receive(slot, ext, ext, NEAR)
    sides = (pl.ds(own, 2), pl.ds(0, rows))
    far_ext[sides] = route_ext[sides]

    right = lax.broadcasted_iota(jnp.int32, (SUB, LANES), 1) < LANES // 2

    def banded(ext, v):
        def part(c):
            return ext[c, pl.ds(v, SUB, stride=bands), :]

        blocks = [part(c) for c in range(own)]
        blocks.append(jnp.where(right, part(own), part(own + 1)))
        return jnp.concatenate(blocks, axis=1)

    for v in range(bands):
        acc[v] = banded(depth_ext, v)
        rain[v] = banded(rain_ext, v)
        coef[v] = banded(coef_ext, v)

    def above(v, get):
        return get(v - 1) if v else pltpu.roll(get(bands - 1), 1, 0)

    def below(v, get):
        return get(v + 1) if v < bands - 1 else pltpu.roll(get(0), SUB - 1, 0)

    def set_masks(ext):
        def routed(v):
            return banded(ext, v)

        for v in range(bands):
            near = {1: above(v, routed), 0: routed(v), -1: below(v, routed)}
            for k, (di, dj) in enumerate(OFFSETS):
                masks[k, v] = jnp.where(near[di] == k + 1, jnp.float32(1.0), jnp.float32(0.0))

    set_masks(route_ext)

    def inflow(v, up, here, down):
        near = {1: up, 0: here, -1: down}
        parts = {}
        for k, (di, dj) in enumerate(OFFSETS):
            term = masks[k, v] * near[di]
            parts[dj] = parts[dj] + term if dj in parts else term
        return parts[0] + (pltpu.roll(parts[1], 1, 1) + pltpu.roll(parts[-1], wide - 1, 1))

    def sweep(field, finish):
        start = field[0]
        up, here = (pltpu.roll(field[bands - 1], 1, 0), start)
        for v in range(bands):
            down = field[v + 1] if v < bands - 1 else pltpu.roll(start, SUB - 1, 0)
            finish(v, inflow(v, up, here, down))
            up, here = here, down

    @pl.loop(0, SUBSTEPS)
    def _(step):
        for v in range(bands):
            h = acc[v]
            factor = coef[v] * jnp.exp(jnp.log(h) * jnp.float32(2.0 / 3.0))
            out = h * (factor / (1.0 + factor))
            share[v] = out
            level[v] = h + rain[v] - out

        def finish(v, came):
            acc[v] = level[v] + came

        sweep(share, finish)

    def finish(v, came):
        acc[v] = level[v] + came

    def passes(count):
        @pl.loop(0, count)
        def _(index):
            sweep(acc, finish)

    def to_plain(field, dst):
        for v in range(bands):
            value = field[v]
            for c in range(own):
                dst[c, pl.ds(v, SUB, stride=bands), :] = value[:, c * LANES : (c + 1) * LANES]

    sub = lax.broadcasted_iota(jnp.int32, (SUB, LANES), 0)

    lane_part = lax.broadcasted_iota(jnp.int32, (SUB, LANES), 1) // MARGIN

    def corner(group, k):
        dr, dc = OFFSETS[k]
        slot = level_slot + group
        return pltpu.make_async_remote_copy(
            src_ref=pack_out.at[group, k],
            dst_ref=pack_in.at[group, k],
            send_sem=send_sem.at[slot, k],
            recv_sem=recv_sem.at[slot, k],
            device_id=(my_row + dr, my_col + dc),
            device_id_type=MESH,
        )

    def send_corners(group, src):
        for k in corners:
            dr, dc = OFFSETS[k]
            start = 0 if dr < 0 else rows - MARGIN
            block, first = (0, 0) if dc < 0 else (own - 1, LANES - MARGIN)
            packed = None
            for g in range(MARGIN // SUB):
                piece = src[block, pl.ds(start + g * SUB, SUB), :]
                shift = (g * MARGIN - first) % LANES
                piece = pltpu.roll(piece, shift, 1) if shift else piece
                packed = piece if packed is None else jnp.where(lane_part == g, piece, packed)
            pack_out[group, k] = packed
        for k in corners:
            @pl.when(exists(*OFFSETS[k]))
            def _(k=k):
                corner(group, k).start()

    def receive_corners(group, dst):
        for k in corners:
            dr, dc = OFFSETS[k]
            there = exists(-dr, -dc)
            start = rows if dr < 0 else total - MARGIN
            block, first = (own, 0) if dc < 0 else (own + 1, LANES - MARGIN)

            @pl.when(there)
            def _(k=k, start=start, block=block, first=first):
                corner(group, k).wait_recv()
                packed = pack_in[group, k]
                for g in range(MARGIN // SUB):
                    shift = (first - g * MARGIN) % LANES
                    piece = pltpu.roll(packed, shift, 1) if shift else packed
                    dst[block, pl.ds(start + g * SUB, SUB), :] = piece

            @pl.when(jnp.logical_not(there))
            def _(start=start, block=block):
                dst[block, pl.ds(start, MARGIN), :] = jnp.zeros((MARGIN, LANES), dst.dtype)

    def widen(src, dst, group, meanwhile, fields):
        slot = level_slot + group
        to_plain(acc, src)
        send_corners(group, src)
        send(slot, src, dst, MARGIN, straight)
        meanwhile()
        receive(slot, src, dst, MARGIN, straight)
        receive_corners(group, dst)
        for v in range(bands):
            inner = sub * bands + v < rows
            for c in range(own):
                at = pl.ds(c * LANES, LANES)
                value = jnp.where(inner, acc[v, :, at], dst[c, pl.ds(v, SUB, stride=bands), :])
                for field in fields:
                    field[v, :, at] = value
            value = jnp.where(
                right,
                dst[own, pl.ds(v, SUB, stride=bands), :],
                dst[own + 1, pl.ds(v, SUB, stride=bands), :],
            )
            for field in fields:
                field[v, :, pl.ds(cols, LANES)] = value

    def in_flight():
        for c in range(own):
            level_ref[:, pl.ds(c * LANES, LANES)] = plain[0, c, pl.ds(0, rows), :]
        receive(far_slot, far_ext, far_ext, MARGIN, slanted)
        set_masks(far_ext)

    widen(plain.at[0], acc_ext.at[0], 0, in_flight, (acc, level))
    passes(MARGIN)
    for group in range(1, GROUPS):
        widen(plain.at[group], acc_ext.at[group], group, lambda: None, (acc,))
        passes(MARGIN)

    to_plain(acc, plain.at[GROUPS])
    for c in range(own):
        discharge_ref[:, pl.ds(c * LANES, LANES)] = jnp.log(1.0 + plain[GROUPS, c, pl.ds(0, rows), :])
    for slot, ext in enumerate(firsts):
        sent_out(slot, ext, ext, NEAR)
    sent_out(far_slot, far_ext, far_ext, MARGIN, slanted)
    for group in range(GROUPS):
        sent_out(level_slot + group, plain.at[group], acc_ext.at[group], MARGIN, straight)
        for k in corners:
            @pl.when(exists(*OFFSETS[k]))
            def _(group=group, k=k):
                corner(group, k).wait_send()


def solution(mesh):
    row_peers, col_peers = mesh.shape["row"], mesh.shape["col"]

    def on_device(depth, rainfall, conveyance, flow_dir, outlet):
        rows, cols = depth.shape
        total = rows + 2 * MARGIN + SPARE
        bands = total // SUB
        wide = cols + LANES
        slots = 5 + GROUPS
        own = cols // LANES
        ext = (own + 2, total, LANES)
        field = (bands, SUB, wide)
        vmem = pl.BlockSpec(memory_space=pltpu.VMEM)
        f32 = jnp.float32
        return pl.pallas_call(
            functools.partial(kernel, row_peers, col_peers),
            out_shape=(jax.ShapeDtypeStruct((rows, cols), f32),) * 2,
            in_specs=[vmem] * 5,
            out_specs=(vmem, vmem),
            scratch_shapes=[
                pltpu.VMEM(ext, f32),
                pltpu.VMEM(ext, f32),
                pltpu.VMEM(ext, f32),
                pltpu.VMEM(ext, jnp.int32),
                pltpu.VMEM(ext, jnp.int32),
                pltpu.VMEM((GROUPS,) + ext, f32),
                pltpu.VMEM((GROUPS + 1, own, total, LANES), f32),
                pltpu.VMEM((GROUPS, len(OFFSETS), SUB, LANES), f32),
                pltpu.VMEM((GROUPS, len(OFFSETS), SUB, LANES), f32),
                pltpu.VMEM(field, f32),
                pltpu.VMEM(field, f32),
                pltpu.VMEM(field, f32),
                pltpu.VMEM(field, f32),
                pltpu.VMEM(field, f32),
                pltpu.VMEM((len(OFFSETS),) + field, f32),
                pltpu.SemaphoreType.DMA((slots, len(OFFSETS))),
                pltpu.SemaphoreType.DMA((slots, len(OFFSETS))),
            ],
            compiler_params=pltpu.CompilerParams(collective_id=0, has_side_effects=True),
        )(depth, rainfall, conveyance, flow_dir, outlet)

    placed = P("row", "col")
    return jax.shard_map(
        on_device,
        mesh=mesh,
        in_specs=(placed,) * 5,
        out_specs=(placed, placed),
        check_vma=False,
    )
```

profile of v0, /device:TPU:0, one launch (start us, length us, event | category | flops | bytes accessed | tf_op | source)
XLA Modules:
  0.0 45.8 jit_solution(10790626064781495231)
XLA Ops:
  0.6 42.9 %shard_map.68 = (f32[64,512]{1,0:T(8,128)}, f32[64,512]{1,0:T(8,128)}) custom-call(f32[64,512]{1,0:T(8,128)} %depth_ref.1, f32[64,512]{1,0:T(8,128)} %rain_ref.1, f32[64,512]{1,0:T(8,128)} %conv_ref.1, s32[64,512]{1,0:T(8,128)} %dir_ref.1, s32[64,512]{1,0:T(8,128)} %outlet_ref.1), custom_call_target="tpu_custom_call" | custom-call | tf_op jit(solution)/shard_map/pallas_call | solution.py:333
  43.5 0.0 copy-start
  43.5 1.6 %copy.9 = f32[64,512]{1,0:T(8,128)} copy(f32[64,512]{1,0:T(8,128)} %get-tuple-element.4) | data formatting | bytes 262144
  45.1 0.0 copy-done
  45.1 0.7 %copy.10 = f32[64,512]{1,0:T(8,128)} copy(f32[64,512]{1,0:T(8,128)S(1)} %copy-done) | data formatting | bytes 262144
Async XLA Ops:
  43.5 1.6 %copy-start = (f32[64,512]{1,0:T(8,128)S(1)}, f32[64,512]{1,0:T(8,128)}, u32[]{:S(2)}) copy-start(f32[64,512]{1,0:T(8,128)} %get-tuple-element.5) | copy-start | bytes 393220
where the time goes:
time: 45.9 us; the launch traced here: 45.8 us
  Pallas kernels  42.9 us (93%)
  local copies, waits for them, and re-layouts  2.26 us (5%)
  between operations  0.65 us (1%)
    pallas_call x1, Pallas kernels, on_device(): pl.pallas_call(functools.partial(kernel, row_peers, col_peers), out_shape...  42.9 us
    unnamed x4, local copies, waits for them, and re-layouts  2.26 us

commit v1 on v0

--- a/solution.py
+++ b/solution.py
@@ -16,18 +16,21 @@
 MARGIN = 32
 GROUPS = PASSES // MARGIN
 SPARE = 0
+VMEM_BYTES = 40 * 1024 * 1024
 MESH = pl.DeviceIdType.MESH
 
 
 def kernel(
     row_peers, col_peers,
-    depth_ref, rain_ref, conv_ref, dir_ref, outlet_ref,
-    level_ref, discharge_ref,
+    depth_hbm, rain_hbm, conv_hbm, dir_hbm, outlet_hbm,
+    out_ref,
+    depth_ref, rain_ref, conv_ref, dir_ref, outlet_ref, load_sem,
     depth_ext, rain_ext, coef_ext, route_ext, far_ext, acc_ext, plain, pack_out, pack_in,
     acc, rain, coef, level, share, masks,
     send_sem, recv_sem,
 ):
     rows, cols = depth_ref.shape
+    level_ref, discharge_ref = out_ref.at[0], out_ref.at[1]
     total = depth_ext.shape[1]
     bands = total // SUB
     wide = cols + LANES
@@ -105,6 +108,15 @@
             pl.semaphore_signal(
                 barrier, inc=1, device_id=(my_row + dr, my_col + dc), device_id_type=MESH
             )
+    staged = (
+        (depth_hbm, depth_ref), (rain_hbm, rain_ref), (conv_hbm, conv_ref),
+        (dir_hbm, dir_ref), (outlet_hbm, outlet_ref),
+    )
+    loads = [pltpu.make_async_copy(src, dst, load_sem.at[i]) for i, (src, dst) in enumerate(staged)]
+    for load in loads:
+        load.start()
+    for load in loads:
+        load.wait()
     for c in range(own):
         at = pl.ds(c * LANES, LANES)
         mine = pl.ds(0, rows)
@@ -330,12 +342,20 @@
         field = (bands, SUB, wide)
         vmem = pl.BlockSpec(memory_space=pltpu.VMEM)
         f32 = jnp.float32
-        return pl.pallas_call(
+        hbm = pl.BlockSpec(memory_space=pltpu.HBM)
+        tile = (rows, cols)
+        both = pl.pallas_call(
             functools.partial(kernel, row_peers, col_peers),
-            out_shape=(jax.ShapeDtypeStruct((rows, cols), f32),) * 2,
-            in_specs=[vmem] * 5,
-            out_specs=(vmem, vmem),
+            out_shape=jax.ShapeDtypeStruct((2, rows, cols), f32),
+            in_specs=[hbm] * 5,
+            out_specs=vmem,
             scratch_shapes=[
+                pltpu.VMEM(tile, f32),
+                pltpu.VMEM(tile, f32),
+                pltpu.VMEM(tile, f32),
+                pltpu.VMEM(tile, jnp.int32),
+                pltpu.VMEM(tile, jnp.int32),
+                pltpu.SemaphoreType.DMA((5,)),
                 pltpu.VMEM(ext, f32),
                 pltpu.VMEM(ext, f32),
                 pltpu.VMEM(ext, f32),
@@ -354,8 +374,14 @@
                 pltpu.SemaphoreType.DMA((slots, len(OFFSETS))),
                 pltpu.SemaphoreType.DMA((slots, len(OFFSETS))),
             ],
-            compiler_params=pltpu.CompilerParams(collective_id=0, has_side_effects=True),
-        )(depth, rainfall, conveyance, flow_dir, outlet)
+            compiler_params=pltpu.CompilerParams(
+                collective_id=0, has_side_effects=True, vmem_limit_bytes=VMEM_BYTES
+            ),
+        )(*(
+            pltpu.with_memory_space_constraint(a, pltpu.HBM)
+            for a in (depth, rainfall, conveyance, flow_dir, outlet)
+        ))
+        return both[0], both[1]
 
     placed = P("row", "col")
     return jax.shard_map(

time: 45.9 us -> 42.6 us (0.928)
  Pallas kernels: 42.9 us -> 41.1 us
  local copies, waits for them, and re-layouts: 2.26 us -> 0.72 us
    unnamed x4 -> x0, local copies, waits for them, and re-layouts: 2.26 us -> none
    pallas_call x1, Pallas kernels: 42.9 us -> 41.1 us  [on_device(): pl.pallas_call(functools.partial(kernel, row_peers, col_peers), out_shape...]
    squeeze x0 -> x1, local copies, waits for them, and re-layouts: none -> 0.72 us  [on_device(): return (both[0], both[1])]
where the time goes in v1:
time: 42.6 us; the launch traced here: 42.5 us
  Pallas kernels  41.1 us (96%)
  local copies, waits for them, and re-layouts  0.72 us (2%)
  between operations  0.64 us (2%)
    pallas_call x1, Pallas kernels, on_device(): pl.pallas_call(functools.partial(kernel, row_peers, col_peers), out_shape...  41.1 us

profile of v1, /device:TPU:0, one launch (start us, length us, event | category | flops | bytes accessed | tf_op | source)
XLA Modules:
  0.0 42.5 jit_solution(6896936303971876292)
XLA Ops:
  0.6 41.1 %shard_map.68 = f32[2,64,512]{2,1,0:T(8,128)S(1)} custom-call(f32[64,512]{1,0:T(8,128)} %depth_hbm.1, f32[64,512]{1,0:T(8,128)} %rain_hbm.1, f32[64,512]{1,0:T(8,128)} %conv_hbm.1, s32[64,512]{1,0:T(8,128)} %dir_hbm.1, s32[64,512]{1,0:T(8,128)} %outlet_hbm.1), custom_call_target="tpu_custom_call" | custom-call | tf_op jit(solution)/shard_map/pallas_call | solution.py:347
  41.7 0.7 %slice_bitcast_fusion = (f32[64,512]{1,0:T(8,128)}, f32[64,512]{1,0:T(8,128)}) fusion(f32[2,64,512]{2,1,0:T(8,128)S(1)} %shard_map.68), kind=kLoop, calls=%fused_computation | loop fusion | bytes 524288 | tf_op jit(solution)/shard_map/squeeze | solution.py:384

commit v2 on v1

--- a/solution.py
+++ b/solution.py
@@ -16,6 +16,8 @@
 MARGIN = 32
 GROUPS = PASSES // MARGIN
 SPARE = 0
+HALF = LANES // 2
+REACH = 3
 VMEM_BYTES = 40 * 1024 * 1024
 MESH = pl.DeviceIdType.MESH
 
@@ -328,6 +330,364 @@
                 corner(group, k).wait_send()
 
 
+def strip_kernel(
+    row_peers, col_peers,
+    depth_hbm, rain_hbm, conv_hbm, dir_hbm, outlet_hbm,
+    out_ref,
+    conv_ref, dir_ref, outlet_ref,
+    near, rows_out, rows_in, plain,
+    h, rain, coef, base, share, near_masks,
+    shifted, window,
+    acc, level, masks, result,
+    load_sem, near_send, near_recv, peer_send, peer_recv,
+):
+    rows, cols = conv_ref.shape
+    own = cols // LANES
+    total = plain.shape[1]
+    thin = total // SUB
+    east, west = own, own + 1
+    wide = cols + 2 * LANES
+    full = row_peers * rows
+    bands = full // SUB
+    span = 2 * LANES
+    f32 = jnp.float32
+    my_row, my_col = lax.axis_index("row"), lax.axis_index("col")
+
+    def exists(dr, dc):
+        r, c = my_row + dr, my_col + dc
+        return (r >= 0) & (r < row_peers) & (c >= 0) & (c < col_peers)
+
+    barrier = pltpu.get_barrier_semaphore()
+
+    def greet(row, col):
+        pl.semaphore_signal(barrier, inc=1, device_id=(row, col), device_id_type=MESH)
+
+    expected = row_peers - 1
+    for dr, dc in OFFSETS:
+        @pl.when(exists(dr, dc))
+        def _(dr=dr, dc=dc):
+            greet(my_row + dr, my_col + dc)
+        if dc:
+            expected = expected + jnp.where(exists(dr, dc), 1, 0)
+    for q in range(row_peers):
+        far = (my_row - q >= 2) | (q - my_row >= 2)
+
+        @pl.when(far)
+        def _(q=q):
+            greet(q, my_col)
+
+    loads = [
+        pltpu.make_async_copy(src, dst, load_sem.at[i])
+        for i, (src, dst) in enumerate(
+            [(conv_hbm, conv_ref), (dir_hbm, dir_ref), (outlet_hbm, outlet_ref)]
+            + [
+                (src.at[:, pl.ds(c * LANES, LANES)], near.at[a, c, pl.ds(0, rows)])
+                for a, src in enumerate((depth_hbm, rain_hbm))
+                for c in range(own)
+            ]
+        )
+    ]
+    for load in loads:
+        load.start()
+    for load in loads:
+        load.wait()
+
+    low = lax.broadcasted_iota(jnp.int32, (SUB, LANES), 1) < HALF
+
+    for c in range(own):
+        at = pl.ds(c * LANES, LANES)
+        code = dir_ref[:, at]
+        near[2, c, pl.ds(0, rows)] = conv_ref[:, at] * jnp.where(
+            (code & 1) == 1, f32(0.70710678), f32(1.0)
+        )
+        near[3, c, pl.ds(0, rows)] = jnp.where(outlet_ref[:, at] == 1, 0, code + 1).astype(f32)
+
+    for a in range(4):
+        for c in range(own):
+            at = pl.ds((a * own + c) * REACH, REACH)
+            rows_out[0, at] = near[a, c, pl.ds(0, REACH)]
+            rows_out[1, at] = near[a, c, pl.ds(rows - REACH, REACH)]
+
+    def shift_tiles(field, get, blocks):
+        for t in range(rows // SUB):
+            tile = pl.ds(t * SUB, SUB)
+            turned = {}
+            for j in blocks:
+                for c in (j - 1, j):
+                    if c not in turned:
+                        turned[c] = pltpu.roll(get(west if c < 0 else c, tile), HALF, 1)
+                shifted[field, j, tile] = jnp.where(low, turned[j - 1], turned[j])
+
+    def route_tile(c, tile):
+        return near[3, c, tile]
+
+    shift_tiles(0, route_tile, range(1, own))
+
+    def near_ends(k):
+        dr, dc = OFFSETS[k]
+        if dc == 0:
+            part = pl.ds(0, 4 * own * REACH)
+            src, dst = (
+                (rows_out.at[0, part], rows_in.at[1, part])
+                if dr < 0
+                else (rows_out.at[1, part], rows_in.at[0, part])
+            )
+        else:
+            rs, rd = {
+                0: (pl.ds(0, rows), pl.ds(0, rows)),
+                -1: (pl.ds(0, SUB), pl.ds(rows, SUB)),
+                1: (pl.ds(rows - SUB, SUB), pl.ds(total - SUB, SUB)),
+            }[dr]
+            src = near.at[:, 0 if dc < 0 else own - 1, rs]
+            dst = near.at[:, east if dc < 0 else west, rd]
+        return src, dst
+
+    def near_copy(k):
+        dr, dc = OFFSETS[k]
+        src, dst = near_ends(k)
+        return pltpu.make_async_remote_copy(
+            src_ref=src, dst_ref=dst, send_sem=near_send.at[k], recv_sem=near_recv.at[k],
+            device_id=(my_row + dr, my_col + dc), device_id_type=MESH,
+        )
+
+    def window_copy(field, half, q):
+        peer = lax.rem(my_row + q, row_peers)
+        return pltpu.make_async_remote_copy(
+            src_ref=shifted.at[field, peer + half],
+            dst_ref=window.at[field, half, pl.ds(pl.multiple_of(my_row * rows, rows), rows)],
+            send_sem=peer_send.at[field, half, q], recv_sem=peer_recv.at[field, half, q],
+            device_id=(peer, my_col), device_id_type=MESH,
+        )
+
+    def send_window(field, early, late):
+        for q in range(1, row_peers):
+            peer = lax.rem(my_row + q, row_peers)
+            for half in (0, 1):
+                edge = peer == (0, row_peers - 1)[half]
+                if early and late:
+                    window_copy(field, half, q).start()
+                else:
+                    @pl.when(edge if late else jnp.logical_not(edge))
+                    def _(half=half, q=q):
+                        window_copy(field, half, q).start()
+        if late:
+            window[field, :, pl.ds(pl.multiple_of(my_row * rows, rows), rows)] = shifted[
+                field, pl.ds(my_row, 2)
+            ]
+
+    def receive_window(field):
+        for q in range(1, row_peers):
+            for half in (0, 1):
+                window_copy(field, half, q).wait_recv()
+
+    def window_sent(field):
+        for q in range(1, row_peers):
+            for half in (0, 1):
+                window_copy(field, half, q).wait_send()
+
+    order = (1, 3, 5, 7, 2, 6, 0, 4)
+    pl.semaphore_wait(barrier, expected)
+    for k in order:
+        @pl.when(exists(*OFFSETS[k]))
+        def _(k=k):
+            near_copy(k).start()
+    send_window(0, True, False)
+
+    blank = pl.ds(rows + REACH, total - rows - 2 * REACH)
+    near[:, pl.ds(0, own), blank] = jnp.zeros((4, own, total - rows - 2 * REACH, LANES), f32)
+
+    for k in order:
+        dr, dc = OFFSETS[k]
+        there = exists(-dr, -dc)
+
+        @pl.when(there)
+        def _(k=k):
+            near_copy(k).wait_recv()
+
+        @pl.when(jnp.logical_not(there))
+        def _(k=k):
+            dst = near_ends(k)[1]
+            dst[...] = jnp.zeros(dst.shape, f32)
+
+    for a in range(4):
+        for c in range(own):
+            at = pl.ds((a * own + c) * REACH, REACH)
+            near[a, c, pl.ds(rows, REACH)] = rows_in[1, at]
+            near[a, c, pl.ds(total - REACH, REACH)] = rows_in[0, at]
+
+    shift_tiles(0, route_tile, (0, own))
+    send_window(0, False, True)
+
+    def near_band(a, v):
+        take = pl.ds(v, SUB, stride=thin)
+        return jnp.concatenate([near[a, c, take, :] for c in range(own + 2)], axis=1)
+
+    for v in range(thin):
+        h[v] = near_band(0, v)
+        rain[v] = near_band(1, v)
+        coef[v] = near_band(2, v)
+        base[v] = near_band(3, v)
+
+    def mask_rows(dst, count, up, here, down):
+        for v in range(count):
+            rows_near = {1: up(v), 0: here(v), -1: down(v)}
+            for k, (di, dj) in enumerate(OFFSETS):
+                dst[k, v] = jnp.where(rows_near[di] == k + 1, f32(1.0), f32(0.0))
+
+    mask_rows(
+        near_masks, thin,
+        lambda v: base[v - 1] if v else pltpu.roll(base[thin - 1], 1, 0),
+        lambda v: base[v],
+        lambda v: base[v + 1] if v < thin - 1 else pltpu.roll(base[0], SUB - 1, 0),
+    )
+
+    def sweep(field, mask, count, width, finish):
+        start = field[0]
+        up, here = pltpu.roll(field[count - 1], 1, 0), start
+        for v in range(count):
+            down = field[v + 1] if v < count - 1 else pltpu.roll(start, SUB - 1, 0)
+            rows_near = {1: up, 0: here, -1: down}
+            parts = {}
+            for k, (di, dj) in enumerate(OFFSETS):
+                term = mask[k, v] * rows_near[di]
+                parts[dj] = parts[dj] + term if dj in parts else term
+            finish(
+                v, parts[0] + (pltpu.roll(parts[1], 1, 1) + pltpu.roll(parts[-1], width - 1, 1))
+            )
+            up, here = here, down
+
+    @pl.loop(0, SUBSTEPS)
+    def _(step):
+        for v in range(thin):
+            depth = h[v]
+            factor = coef[v] * jnp.exp(jnp.log(depth) * f32(2.0 / 3.0))
+            out = depth * (factor / (1.0 + factor))
+            share[v] = out
+            base[v] = depth + rain[v] - out
+
+        def finish(v, came):
+            h[v] = base[v] + came
+
+        sweep(share, near_masks, thin, wide, finish)
+
+    for v in range(thin):
+        value = h[v]
+        for c in range(own + 2):
+            plain[c, pl.ds(v, SUB, stride=thin), :] = value[:, c * LANES : (c + 1) * LANES]
+    shift_tiles(1, lambda c, tile: plain[c, tile], range(own + 1))
+    send_window(1, True, True)
+    for c in range(own):
+        out_ref[0, :, pl.ds(c * LANES, LANES)] = plain[c, pl.ds(0, rows)]
+
+    def band(field, v):
+        take = pl.ds(v, SUB, stride=bands)
+        return jnp.concatenate([window[field, 0, take, :], window[field, 1, take, :]], axis=1)
+
+    sub = lax.broadcasted_iota(jnp.int32, (SUB, span), 0)
+    receive_window(0)
+    for v in range(bands):
+        level[v] = band(0, v)
+    mask_rows(
+        masks, bands,
+        lambda v: level[v - 1] if v else jnp.where(
+            sub == 0, f32(0.0), pltpu.roll(level[bands - 1], 1, 0)
+        ),
+        lambda v: level[v],
+        lambda v: level[v + 1] if v < bands - 1 else jnp.where(
+            sub == SUB - 1, f32(0.0), pltpu.roll(level[0], SUB - 1, 0)
+        ),
+    )
+    receive_window(1)
+    for v in range(bands):
+        value = band(1, v)
+        level[v] = value
+        acc[v] = value
+
+    def finish(v, came):
+        acc[v] = level[v] + came
+
+    @pl.loop(0, PASSES)
+    def _(index):
+        sweep(acc, masks, bands, span, finish)
+
+    for v in range(bands):
+        value = acc[v]
+        core = jnp.where(
+            low, pltpu.roll(value[:, :LANES], HALF, 1), pltpu.roll(value[:, LANES:], HALF, 1)
+        )
+        result[pl.ds(v, SUB, stride=bands), :] = jnp.log(1.0 + core)
+
+    mine = pl.ds(pl.multiple_of(my_row * LANES, LANES), LANES)
+
+    def result_copy(q):
+        peer = lax.rem(my_row + q, row_peers)
+        return pltpu.make_async_remote_copy(
+            src_ref=result.at[pl.ds(pl.multiple_of(peer * rows, rows), rows)],
+            dst_ref=out_ref.at[1, :, mine],
+            send_sem=peer_send.at[2, 0, q], recv_sem=peer_recv.at[2, 0, q],
+            device_id=(peer, my_col), device_id_type=MESH,
+        )
+
+    for q in range(1, row_peers):
+        result_copy(q).start()
+    out_ref[1, :, mine] = result[pl.ds(pl.multiple_of(my_row * rows, rows), rows)]
+    for k in order:
+        @pl.when(exists(*OFFSETS[k]))
+        def _(k=k):
+            near_copy(k).wait_send()
+    window_sent(0)
+    window_sent(1)
+    for q in range(1, row_peers):
+        result_copy(q).wait_recv()
+    for q in range(1, row_peers):
+        result_copy(q).wait_send()
+
+
+def strip_call(row_peers, col_peers, rows, cols):
+    own = cols // LANES
+    total = rows + 2 * SUB
+    thin, bands = total // SUB, row_peers * rows // SUB
+    f32, i32 = jnp.float32, jnp.int32
+    tile = (rows, cols)
+    slim = (thin, SUB, cols + 2 * LANES)
+    field = (bands, SUB, 2 * LANES)
+    return pl.pallas_call(
+        functools.partial(strip_kernel, row_peers, col_peers),
+        out_shape=jax.ShapeDtypeStruct((2, rows, cols), f32),
+        in_specs=[pl.BlockSpec(memory_space=pltpu.HBM)] * 5,
+        out_specs=pl.BlockSpec(memory_space=pltpu.VMEM),
+        scratch_shapes=[
+            pltpu.VMEM(tile, f32),
+            pltpu.VMEM(tile, i32),
+            pltpu.VMEM(tile, i32),
+            pltpu.VMEM((4, own + 2, total + SUB, LANES), f32),
+            pltpu.VMEM((2, 4 * own * REACH + SUB, LANES), f32),
+            pltpu.VMEM((2, 4 * own * REACH + SUB, LANES), f32),
+            pltpu.VMEM((own + 2, total, LANES), f32),
+            pltpu.VMEM(slim, f32),
+            pltpu.VMEM(slim, f32),
+            pltpu.VMEM(slim, f32),
+            pltpu.VMEM(slim, f32),
+            pltpu.VMEM(slim, f32),
+            pltpu.VMEM((len(OFFSETS),) + slim, f32),
+            pltpu.VMEM((2, own + 1, rows, LANES), f32),
+            pltpu.VMEM((2, 2, row_peers * rows, LANES), f32),
+            pltpu.VMEM(field, f32),
+            pltpu.VMEM(field, f32),
+            pltpu.VMEM((len(OFFSETS),) + field, f32),
+            pltpu.VMEM((row_peers * rows, LANES), f32),
+            pltpu.SemaphoreType.DMA((3 + 2 * own,)),
+            pltpu.SemaphoreType.DMA((len(OFFSETS),)),
+            pltpu.SemaphoreType.DMA((len(OFFSETS),)),
+            pltpu.SemaphoreType.DMA((3, 2, row_peers)),
+            pltpu.SemaphoreType.DMA((3, 2, row_peers)),
+        ],
+        compiler_params=pltpu.CompilerParams(
+            collective_id=0, has_side_effects=True, vmem_limit_bytes=VMEM_BYTES
+        ),
+    )
+
+
 def solution(mesh):
     row_peers, col_peers = mesh.shape["row"], mesh.shape["col"]
 
@@ -342,6 +702,13 @@
         field = (bands, SUB, wide)
         vmem = pl.BlockSpec(memory_space=pltpu.VMEM)
         f32 = jnp.float32
+        args = tuple(
+            pltpu.with_memory_space_constraint(a, pltpu.HBM)
+            for a in (depth, rainfall, conveyance, flow_dir, outlet)
+        )
+        if cols == row_peers * LANES and row_peers > 1 and rows % (2 * SUB) == 0 and PASSES <= HALF:
+            both = strip_call(row_peers, col_peers, rows, cols)(*args)
+            return both[0], both[1]
         hbm = pl.BlockSpec(memory_space=pltpu.HBM)
         tile = (rows, cols)
         both = pl.pallas_call(
@@ -377,10 +744,7 @@
             compiler_params=pltpu.CompilerParams(
                 collective_id=0, has_side_effects=True, vmem_limit_bytes=VMEM_BYTES
             ),
-        )(*(
-            pltpu.with_memory_space_constraint(a, pltpu.HBM)
-            for a in (depth, rainfall, conveyance, flow_dir, outlet)
-        ))
+        )(*args)
         return both[0], both[1]
 
     placed = P("row", "col")

time: 42.6 us -> 34.5 us (0.81)
  Pallas kernels: 41.1 us -> 33 us
    pallas_call x1, Pallas kernels: 41.1 us -> 33 us  [on_device(): both = strip_call(row_peers, col_peers, rows, cols)(*args)]
where the time goes in v2:
time: 34.5 us; the launch traced here: 34.4 us
  Pallas kernels  33 us (96%)
  local copies, waits for them, and re-layouts  0.72 us (2%)
  between operations  0.64 us (2%)
    pallas_call x1, Pallas kernels, on_device(): both = strip_call(row_peers, col_peers, rows, cols)(*args)  33 us
    squeeze x1, local copies, waits for them, and re-layouts, on_device(): return (both[0], both[1])  0.72 us

profile of v2, /device:TPU:0, one launch (start us, length us, event | category | flops | bytes accessed | tf_op | source)
XLA Modules:
  0.0 34.4 jit_solution(14392963476565929157)
XLA Ops:
  0.6 33.0 %shard_map.68 = f32[2,64,512]{2,1,0:T(8,128)S(1)} custom-call(f32[64,512]{1,0:T(8,128)} %depth_hbm.1, f32[64,512]{1,0:T(8,128)} %rain_hbm.1, f32[64,512]{1,0:T(8,128)} %conv_hbm.1, s32[64,512]{1,0:T(8,128)} %dir_hbm.1, s32[64,512]{1,0:T(8,128)} %outlet_hbm.1), custom_call_target="tpu_custom_call" | custom-call | tf_op jit(solution)/shard_map/pallas_call | solution.py:710
  33.7 0.7 %slice_bitcast_fusion = (f32[64,512]{1,0:T(8,128)}, f32[64,512]{1,0:T(8,128)}) fusion(f32[2,64,512]{2,1,0:T(8,128)S(1)} %shard_map.68), kind=kLoop, calls=%fused_computation | loop fusion | bytes 524288 | tf_op jit(solution)/shard_map/squeeze | solution.py:711

commit v3 on v2

--- a/solution.py
+++ b/solution.py
@@ -338,7 +338,7 @@
     near, rows_out, rows_in, plain,
     h, rain, coef, base, share, near_masks,
     shifted, window,
-    acc, level, masks, result,
+    acc, level, masks, hold, tall, result,
     load_sem, near_send, near_recv, peer_send, peer_recv,
 ):
     rows, cols = conv_ref.shape
@@ -347,9 +347,8 @@
     thin = total // SUB
     east, west = own, own + 1
     wide = cols + 2 * LANES
-    full = row_peers * rows
-    bands = full // SUB
     span = 2 * LANES
+    bands = span // SUB
     f32 = jnp.float32
     my_row, my_col = lax.axis_index("row"), lax.axis_index("col")
 
@@ -579,43 +578,92 @@
     for c in range(own):
         out_ref[0, :, pl.ds(c * LANES, LANES)] = plain[c, pl.ds(0, rows)]
 
-    def band(field, v):
-        take = pl.ds(v, SUB, stride=bands)
-        return jnp.concatenate([window[field, 0, take, :], window[field, 1, take, :]], axis=1)
-
-    sub = lax.broadcasted_iota(jnp.int32, (SUB, span), 0)
+    def lay(field):
+        for b in (0, 1):
+            for half in (0, 1):
+                tall[b, pl.ds(half * LANES, LANES), :] = window[
+                    field, half, pl.ds(b, LANES, stride=2), :
+                ].T
+
+    def band(v, b):
+        return tall[b, pl.ds(v, SUB, stride=bands), :]
+
+    along = lax.broadcasted_iota(jnp.int32, (SUB, LANES), 1)
     receive_window(0)
+    lay(0)
+    for b in (0, 1):
+        for v in range(bands):
+            cols_near = {
+                1: band(v - 1, b) if v else pltpu.roll(band(bands - 1, b), 1, 0),
+                0: band(v, b),
+                -1: band(v + 1, b) if v < bands - 1 else pltpu.roll(band(0, b), SUB - 1, 0),
+            }
+            for k, (di, dj) in enumerate(OFFSETS):
+                here = cols_near[dj] == k + 1
+                if (di, b) == (1, 1):
+                    here = here & (along < LANES - 1)
+                elif (di, b) == (-1, 0):
+                    here = here & (along > 0)
+                masks[k, v, b] = jnp.where(here, f32(1.0), f32(0.0))
+    receive_window(1)
+    lay(1)
     for v in range(bands):
-        level[v] = band(0, v)
-    mask_rows(
-        masks, bands,
-        lambda v: level[v - 1] if v else jnp.where(
-            sub == 0, f32(0.0), pltpu.roll(level[bands - 1], 1, 0)
-        ),
-        lambda v: level[v],
-        lambda v: level[v + 1] if v < bands - 1 else jnp.where(
-            sub == SUB - 1, f32(0.0), pltpu.roll(level[0], SUB - 1, 0)
-        ),
-    )
-    receive_window(1)
+        for b in (0, 1):
+            value = band(v, b)
+            level[v, b] = value
+            acc[v, b] = value
+
+    def pair(ref, v):
+        return ref[v, 0], ref[v, 1]
+
+    def turn(values, amount):
+        return tuple(pltpu.roll(value, amount, 0) for value in values)
+
+    def gather(held, seed, left, here, right):
+        cols_near = {1: left, 0: here, -1: right}
+        parts = {}
+        for k, (di, dj) in enumerate(OFFSETS):
+            for b in (0, 1):
+                term = held[k, b] * cols_near[dj][b]
+                parts[di, b] = parts[di, b] + term if (di, b) in parts else term
+        return (
+            seed[0] + (parts[0, 0] + (parts[-1, 1] + pltpu.roll(parts[1, 1], 1, 1))),
+            seed[1] + (parts[0, 1] + (parts[1, 0] + pltpu.roll(parts[-1, 0], LANES - 1, 1))),
+        )
+
+    def fetch(v):
+        return {(k, b): masks[k, v, b] for k in range(len(OFFSETS)) for b in (0, 1)}
+
+    def put(ref, v, values):
+        ref[v, 0], ref[v, 1] = values
+
+    @pl.loop(0, PASSES // 2)
+    def _(index):
+        left, here = turn(pair(acc, bands - 1), 1), pair(acc, 0)
+        older = newer = held = seed = None
+        for v in range(bands):
+            right = pair(acc, v + 1) if v < bands - 1 else turn(pair(acc, 0), SUB - 1)
+            fresh, start = fetch(v), pair(level, v)
+            value = gather(fresh, start, left, here, right)
+            if v < 2:
+                put(hold, v, value)
+            else:
+                put(acc, v - 1, gather(held, seed, older, newer, value))
+            older, newer = newer, value
+            held, seed = fresh, start
+            left, here = here, right
+        put(acc, bands - 1, gather(held, seed, older, newer, turn(pair(hold, 0), SUB - 1)))
+        put(
+            acc, 0,
+            gather(fetch(0), pair(level, 0), turn(newer, 1), pair(hold, 0), pair(hold, 1)),
+        )
+
     for v in range(bands):
-        value = band(1, v)
-        level[v] = value
-        acc[v] = value
-
-    def finish(v, came):
-        acc[v] = level[v] + came
-
-    @pl.loop(0, PASSES)
-    def _(index):
-        sweep(acc, masks, bands, span, finish)
-
-    for v in range(bands):
-        value = acc[v]
-        core = jnp.where(
-            low, pltpu.roll(value[:, :LANES], HALF, 1), pltpu.roll(value[:, LANES:], HALF, 1)
-        )
-        result[pl.ds(v, SUB, stride=bands), :] = jnp.log(1.0 + core)
+        for b in (0, 1):
+            tall[b, pl.ds(v, SUB, stride=bands), :] = acc[v, b]
+    for b in (0, 1):
+        core = jnp.log(1.0 + tall[b, pl.ds(HALF, LANES), :])
+        result[pl.ds(b, LANES, stride=2), :] = core.T
 
     mine = pl.ds(pl.multiple_of(my_row * LANES, LANES), LANES)
 
@@ -646,11 +694,11 @@
 def strip_call(row_peers, col_peers, rows, cols):
     own = cols // LANES
     total = rows + 2 * SUB
-    thin, bands = total // SUB, row_peers * rows // SUB
+    thin, bands = total // SUB, 2 * LANES // SUB
     f32, i32 = jnp.float32, jnp.int32
     tile = (rows, cols)
     slim = (thin, SUB, cols + 2 * LANES)
-    field = (bands, SUB, 2 * LANES)
+    field = (bands, 2, SUB, LANES)
     return pl.pallas_call(
         functools.partial(strip_kernel, row_peers, col_peers),
         out_shape=jax.ShapeDtypeStruct((2, rows, cols), f32),
@@ -675,6 +723,8 @@
             pltpu.VMEM(field, f32),
             pltpu.VMEM(field, f32),
             pltpu.VMEM((len(OFFSETS),) + field, f32),
+            pltpu.VMEM((2, 2, SUB, LANES), f32),
+            pltpu.VMEM((2, 2 * LANES, LANES), f32),
             pltpu.VMEM((row_peers * rows, LANES), f32),
             pltpu.SemaphoreType.DMA((3 + 2 * own,)),
             pltpu.SemaphoreType.DMA((len(OFFSETS),)),
@@ -706,7 +756,8 @@
             pltpu.with_memory_space_constraint(a, pltpu.HBM)
             for a in (depth, rainfall, conveyance, flow_dir, outlet)
         )
-        if cols == row_peers * LANES and row_peers > 1 and rows % (2 * SUB) == 0 and PASSES <= HALF:
+        strips = row_peers > 1 and cols == row_peers * LANES and row_peers * rows == 2 * LANES
+        if strips and rows % SUB == 0 and PASSES <= HALF and PASSES % 2 == 0:
             both = strip_call(row_peers, col_peers, rows, cols)(*args)
             return both[0], both[1]
         hbm = pl.BlockSpec(memory_space=pltpu.HBM)

time: 34.5 us -> 31.3 us (0.907)
  Pallas kernels: 33 us -> 29.8 us
    pallas_call x1, Pallas kernels: 33 us -> 29.8 us  [on_device(): both = strip_call(row_peers, col_peers, rows, cols)(*args)]
where the time goes in v3:
time: 31.3 us; the launch traced here: 31.2 us
  Pallas kernels  29.8 us (95%)
  local copies, waits for them, and re-layouts  0.72 us (2%)
  between operations  0.64 us (2%)
    pallas_call x1, Pallas kernels, on_device(): both = strip_call(row_peers, col_peers, rows, cols)(*args)  29.8 us
    squeeze x1, local copies, waits for them, and re-layouts, on_device(): return (both[0], both[1])  0.72 us

profile of v3, /device:TPU:0, one launch (start us, length us, event | category | flops | bytes accessed | tf_op | source)
XLA Modules:
  0.0 31.2 jit_solution(8025660547506902434)
XLA Ops:
  0.6 29.8 %shard_map.68 = f32[2,64,512]{2,1,0:T(8,128)S(1)} custom-call(f32[64,512]{1,0:T(8,128)} %depth_hbm.1, f32[64,512]{1,0:T(8,128)} %rain_hbm.1, f32[64,512]{1,0:T(8,128)} %conv_hbm.1, s32[64,512]{1,0:T(8,128)} %dir_hbm.1, s32[64,512]{1,0:T(8,128)} %outlet_hbm.1), custom_call_target="tpu_custom_call" | custom-call | tf_op jit(solution)/shard_map/pallas_call | solution.py:761
  30.5 0.7 %slice_bitcast_fusion = (f32[64,512]{1,0:T(8,128)}, f32[64,512]{1,0:T(8,128)}) fusion(f32[2,64,512]{2,1,0:T(8,128)S(1)} %shard_map.68), kind=kLoop, calls=%fused_computation | loop fusion | bytes 524288 | tf_op jit(solution)/shard_map/squeeze | solution.py:762

commit v4 on v3

--- a/solution.py
+++ b/solution.py
@@ -18,6 +18,8 @@
 SPARE = 0
 HALF = LANES // 2
 REACH = 3
+PACK = 2 * SUB
+STAGES = (24, 20, 20)
 VMEM_BYTES = 40 * 1024 * 1024
 MESH = pl.DeviceIdType.MESH
 
@@ -330,16 +332,25 @@
                 corner(group, k).wait_send()
 
 
+def stage_plan():
+    left, plan = PASSES, []
+    for count in STAGES:
+        plan.append((count, HALF - left, (LANES + 2 * left) // SUB))
+        left -= count
+    return plan
+
+
 def strip_kernel(
     row_peers, col_peers,
     depth_hbm, rain_hbm, conv_hbm, dir_hbm, outlet_hbm,
     out_ref,
     conv_ref, dir_ref, outlet_ref,
-    near, rows_out, rows_in, plain,
+    near, rows_out, rows_in, corners_in, plain,
     h, rain, coef, base, share, near_masks,
     shifted, window,
-    acc, level, masks, hold, tall, result,
+    acc, level, hold, tall, moved, result,
     load_sem, near_send, near_recv, peer_send, peer_recv,
+    *stage_masks,
 ):
     rows, cols = conv_ref.shape
     own = cols // LANES
@@ -347,8 +358,6 @@
     thin = total // SUB
     east, west = own, own + 1
     wide = cols + 2 * LANES
-    span = 2 * LANES
-    bands = span // SUB
     f32 = jnp.float32
     my_row, my_col = lax.axis_index("row"), lax.axis_index("col")
 
@@ -403,7 +412,7 @@
 
     for a in range(4):
         for c in range(own):
-            at = pl.ds((a * own + c) * REACH, REACH)
+            at = pl.ds((c * 4 + a) * REACH, REACH)
             rows_out[0, at] = near[a, c, pl.ds(0, REACH)]
             rows_out[1, at] = near[a, c, pl.ds(rows - REACH, REACH)]
 
@@ -420,8 +429,6 @@
     def route_tile(c, tile):
         return near[3, c, tile]
 
-    shift_tiles(0, route_tile, range(1, own))
-
     def near_ends(k):
         dr, dc = OFFSETS[k]
         if dc == 0:
@@ -431,14 +438,14 @@
                 if dr < 0
                 else (rows_out.at[1, part], rows_in.at[0, part])
             )
+        elif dr == 0:
+            part = pl.ds(0, rows)
+            src = near.at[:, 0 if dc < 0 else own - 1, part]
+            dst = near.at[:, east if dc < 0 else west, part]
         else:
-            rs, rd = {
-                0: (pl.ds(0, rows), pl.ds(0, rows)),
-                -1: (pl.ds(0, SUB), pl.ds(rows, SUB)),
-                1: (pl.ds(rows - SUB, SUB), pl.ds(total - SUB, SUB)),
-            }[dr]
-            src = near.at[:, 0 if dc < 0 else own - 1, rs]
-            dst = near.at[:, east if dc < 0 else west, rd]
+            part = pl.ds(0 if dc < 0 else 4 * own * REACH - PACK, PACK)
+            src = rows_out.at[0 if dr < 0 else 1, part]
+            dst = corners_in.at[k, pl.ds(0, PACK)]
         return src, dst
 
     def near_copy(k):
@@ -490,10 +497,11 @@
         @pl.when(exists(*OFFSETS[k]))
         def _(k=k):
             near_copy(k).start()
+    shift_tiles(0, route_tile, range(1, own))
     send_window(0, True, False)
 
     blank = pl.ds(rows + REACH, total - rows - 2 * REACH)
-    near[:, pl.ds(0, own), blank] = jnp.zeros((4, own, total - rows - 2 * REACH, LANES), f32)
+    near[:, :, blank] = jnp.zeros((4, own + 2, total - rows - 2 * REACH, LANES), f32)
 
     for k in order:
         dr, dc = OFFSETS[k]
@@ -508,11 +516,18 @@
             dst = near_ends(k)[1]
             dst[...] = jnp.zeros(dst.shape, f32)
 
+    below, above = pl.ds(rows, REACH), pl.ds(total - REACH, REACH)
     for a in range(4):
         for c in range(own):
-            at = pl.ds((a * own + c) * REACH, REACH)
-            near[a, c, pl.ds(rows, REACH)] = rows_in[1, at]
-            near[a, c, pl.ds(total - REACH, REACH)] = rows_in[0, at]
+            at = pl.ds((c * 4 + a) * REACH, REACH)
+            near[a, c, below] = rows_in[1, at]
+            near[a, c, above] = rows_in[0, at]
+        for k in (1, 3, 5, 7):
+            dr, dc = OFFSETS[k]
+            start = 0 if dc < 0 else PACK - 4 * REACH
+            near[a, east if dc < 0 else west, below if dr < 0 else above] = corners_in[
+                k, pl.ds(start + a * REACH, REACH)
+            ]
 
     shift_tiles(0, route_tile, (0, own))
     send_window(0, False, True)
@@ -585,33 +600,31 @@
                     field, half, pl.ds(b, LANES, stride=2), :
                 ].T
 
-    def band(v, b):
-        return tall[b, pl.ds(v, SUB, stride=bands), :]
-
+    def band(ref, first, count, v, b):
+        return ref[b, pl.ds(first + v, SUB, stride=count), :]
+
+    plan = stage_plan()
     along = lax.broadcasted_iota(jnp.int32, (SUB, LANES), 1)
     receive_window(0)
     lay(0)
-    for b in (0, 1):
-        for v in range(bands):
-            cols_near = {
-                1: band(v - 1, b) if v else pltpu.roll(band(bands - 1, b), 1, 0),
-                0: band(v, b),
-                -1: band(v + 1, b) if v < bands - 1 else pltpu.roll(band(0, b), SUB - 1, 0),
-            }
-            for k, (di, dj) in enumerate(OFFSETS):
-                here = cols_near[dj] == k + 1
-                if (di, b) == (1, 1):
-                    here = here & (along < LANES - 1)
-                elif (di, b) == (-1, 0):
-                    here = here & (along > 0)
-                masks[k, v, b] = jnp.where(here, f32(1.0), f32(0.0))
+    for (_, first, count), masks in zip(plan, stage_masks):
+        for b in (0, 1):
+            codes = [band(tall, first, count, v, b) for v in range(count)]
+            for v in range(count):
+                cols_near = {
+                    1: codes[v - 1] if v else pltpu.roll(codes[-1], 1, 0),
+                    0: codes[v],
+                    -1: codes[v + 1] if v < count - 1 else pltpu.roll(codes[0], SUB - 1, 0),
+                }
+                for k, (di, dj) in enumerate(OFFSETS):
+                    here = cols_near[dj] == k + 1
+                    if (di, b) == (1, 1):
+                        here = here & (along < LANES - 1)
+                    elif (di, b) == (-1, 0):
+                        here = here & (along > 0)
+                    masks[k, v, b] = jnp.where(here, f32(1.0), f32(0.0))
     receive_window(1)
     lay(1)
-    for v in range(bands):
-        for b in (0, 1):
-            value = band(v, b)
-            level[v, b] = value
-            acc[v, b] = value
 
     def pair(ref, v):
         return ref[v, 0], ref[v, 1]
@@ -631,38 +644,48 @@
             seed[1] + (parts[0, 1] + (parts[1, 0] + pltpu.roll(parts[-1, 0], LANES - 1, 1))),
         )
 
-    def fetch(v):
-        return {(k, b): masks[k, v, b] for k in range(len(OFFSETS)) for b in (0, 1)}
-
     def put(ref, v, values):
         ref[v, 0], ref[v, 1] = values
 
-    @pl.loop(0, PASSES // 2)
-    def _(index):
-        left, here = turn(pair(acc, bands - 1), 1), pair(acc, 0)
-        older = newer = held = seed = None
-        for v in range(bands):
-            right = pair(acc, v + 1) if v < bands - 1 else turn(pair(acc, 0), SUB - 1)
-            fresh, start = fetch(v), pair(level, v)
-            value = gather(fresh, start, left, here, right)
-            if v < 2:
-                put(hold, v, value)
-            else:
-                put(acc, v - 1, gather(held, seed, older, newer, value))
-            older, newer = newer, value
-            held, seed = fresh, start
-            left, here = here, right
-        put(acc, bands - 1, gather(held, seed, older, newer, turn(pair(hold, 0), SUB - 1)))
-        put(
-            acc, 0,
-            gather(fetch(0), pair(level, 0), turn(newer, 1), pair(hold, 0), pair(hold, 1)),
-        )
-
-    for v in range(bands):
-        for b in (0, 1):
-            tall[b, pl.ds(v, SUB, stride=bands), :] = acc[v, b]
+    def run(passes, masks, count):
+        def fetch(v):
+            return {(k, b): masks[k, v, b] for k in range(len(OFFSETS)) for b in (0, 1)}
+
+        @pl.loop(0, passes // 2)
+        def _(index):
+            left, here = turn(pair(acc, count - 1), 1), pair(acc, 0)
+            older = newer = held = seed = None
+            for v in range(count):
+                right = pair(acc, v + 1) if v < count - 1 else turn(pair(acc, 0), SUB - 1)
+                fresh, start = fetch(v), pair(level, v)
+                value = gather(fresh, start, left, here, right)
+                if v < 2:
+                    put(hold, v, value)
+                else:
+                    put(acc, v - 1, gather(held, seed, older, newer, value))
+                older, newer = newer, value
+                held, seed = fresh, start
+                left, here = here, right
+            put(acc, count - 1, gather(held, seed, older, newer, turn(pair(hold, 0), SUB - 1)))
+            put(
+                acc, 0,
+                gather(fetch(0), pair(level, 0), turn(newer, 1), pair(hold, 0), pair(hold, 1)),
+            )
+
+    source = tall
+    for (passes, first, count), masks in zip(plan, stage_masks):
+        for v in range(count):
+            for b in (0, 1):
+                value = band(tall, first, count, v, b)
+                level[v, b] = value
+                acc[v, b] = value if source is tall else band(source, first, count, v, b)
+        run(passes, masks, count)
+        source = moved
+        for v in range(count):
+            for b in (0, 1):
+                moved[b, pl.ds(first + v, SUB, stride=count), :] = acc[v, b]
     for b in (0, 1):
-        core = jnp.log(1.0 + tall[b, pl.ds(HALF, LANES), :])
+        core = jnp.log(1.0 + moved[b, pl.ds(HALF, LANES), :])
         result[pl.ds(b, LANES, stride=2), :] = core.T
 
     mine = pl.ds(pl.multiple_of(my_row * LANES, LANES), LANES)
@@ -711,6 +734,7 @@
             pltpu.VMEM((4, own + 2, total + SUB, LANES), f32),
             pltpu.VMEM((2, 4 * own * REACH + SUB, LANES), f32),
             pltpu.VMEM((2, 4 * own * REACH + SUB, LANES), f32),
+            pltpu.VMEM((len(OFFSETS), PACK + SUB, LANES), f32),
             pltpu.VMEM((own + 2, total, LANES), f32),
             pltpu.VMEM(slim, f32),
             pltpu.VMEM(slim, f32),
@@ -722,8 +746,8 @@
             pltpu.VMEM((2, 2, row_peers * rows, LANES), f32),
             pltpu.VMEM(field, f32),
             pltpu.VMEM(field, f32),
-            pltpu.VMEM((len(OFFSETS),) + field, f32),
             pltpu.VMEM((2, 2, SUB, LANES), f32),
+            pltpu.VMEM((2, 2 * LANES, LANES), f32),
             pltpu.VMEM((2, 2 * LANES, LANES), f32),
             pltpu.VMEM((row_peers * rows, LANES), f32),
             pltpu.SemaphoreType.DMA((3 + 2 * own,)),
@@ -731,6 +755,10 @@
             pltpu.SemaphoreType.DMA((len(OFFSETS),)),
             pltpu.SemaphoreType.DMA((3, 2, row_peers)),
             pltpu.SemaphoreType.DMA((3, 2, row_peers)),
+        ]
+        + [
+            pltpu.VMEM((len(OFFSETS), count, 2, SUB, LANES), f32)
+            for _, _, count in stage_plan()
         ],
         compiler_params=pltpu.CompilerParams(
             collective_id=0, has_side_effects=True, vmem_limit_bytes=VMEM_BYTES
@@ -757,7 +785,7 @@
             for a in (depth, rainfall, conveyance, flow_dir, outlet)
         )
         strips = row_peers > 1 and cols == row_peers * LANES and row_peers * rows == 2 * LANES
-        if strips and rows % SUB == 0 and PASSES <= HALF and PASSES % 2 == 0:
+        if strips and rows % PACK == 0 and row_peers % 2 == 0:
             both = strip_call(row_peers, col_peers, rows, cols)(*args)
             return both[0], both[1]
         hbm = pl.BlockSpec(memory_space=pltpu.HBM)

time: 31.3 us -> 28.6 us (0.914)
  Pallas kernels: 29.8 us -> 27.1 us
    pallas_call x1, Pallas kernels: 29.8 us -> 27.1 us  [on_device(): both = strip_call(row_peers, col_peers, rows, cols)(*args)]
where the time goes in v4:
time: 28.6 us; the launch traced here: 28.5 us
  Pallas kernels  27.1 us (95%)
  local copies, waits for them, and re-layouts  0.72 us (3%)
  between operations  0.64 us (2%)
    pallas_call x1, Pallas kernels, on_device(): both = strip_call(row_peers, col_peers, rows, cols)(*args)  27.1 us
    squeeze x1, local copies, waits for them, and re-layouts, on_device(): return (both[0], both[1])  0.72 us

profile of v4, /device:TPU:0, one launch (start us, length us, event | category | flops | bytes accessed | tf_op | source)
XLA Modules:
  0.0 28.5 jit_solution(17880709553498267374)
XLA Ops:
  0.6 27.1 %shard_map.68 = f32[2,64,512]{2,1,0:T(8,128)S(1)} custom-call(f32[64,512]{1,0:T(8,128)} %depth_hbm.1, f32[64,512]{1,0:T(8,128)} %rain_hbm.1, f32[64,512]{1,0:T(8,128)} %conv_hbm.1, s32[64,512]{1,0:T(8,128)} %dir_hbm.1, s32[64,512]{1,0:T(8,128)} %outlet_hbm.1), custom_call_target="tpu_custom_call" | custom-call | tf_op jit(solution)/shard_map/pallas_call | solution.py:789
  27.8 0.7 %slice_bitcast_fusion = (f32[64,512]{1,0:T(8,128)}, f32[64,512]{1,0:T(8,128)}) fusion(f32[2,64,512]{2,1,0:T(8,128)S(1)} %shard_map.68), kind=kLoop, calls=%fused_computation | loop fusion | bytes 524288 | tf_op jit(solution)/shard_map/squeeze | solution.py:790

commit v5 on v4

--- a/solution.py
+++ b/solution.py
@@ -345,11 +345,11 @@
     depth_hbm, rain_hbm, conv_hbm, dir_hbm, outlet_hbm,
     out_ref,
     conv_ref, dir_ref, outlet_ref,
-    near, rows_out, rows_in, corners_in, plain,
+    near, sides_in, rows_out, rows_in, corners_in, plain,
     h, rain, coef, base, share, near_masks,
     shifted, window,
     acc, level, hold, tall, moved, result,
-    load_sem, near_send, near_recv, peer_send, peer_recv,
+    load_sem, near_send, near_recv, peer_send, peer_recv, rim_send, rim_recv,
     *stage_masks,
 ):
     rows, cols = conv_ref.shape
@@ -416,8 +416,12 @@
             rows_out[0, at] = near[a, c, pl.ds(0, REACH)]
             rows_out[1, at] = near[a, c, pl.ds(rows - REACH, REACH)]
 
-    def shift_tiles(field, get, blocks):
-        for t in range(rows // SUB):
+    every = range(rows // SUB)
+    rim = (0, rows // SUB - 1)
+    inner = range(1, rows // SUB - 1)
+
+    def shift_tiles(field, get, blocks, tiles=every):
+        for t in tiles:
             tile = pl.ds(t * SUB, SUB)
             turned = {}
             for j in blocks:
@@ -440,8 +444,8 @@
             )
         elif dr == 0:
             part = pl.ds(0, rows)
-            src = near.at[:, 0 if dc < 0 else own - 1, part]
-            dst = near.at[:, east if dc < 0 else west, part]
+            src = near.at[pl.ds(0, 3), 0 if dc < 0 else own - 1, part]
+            dst = sides_in.at[0 if dc < 0 else 1, pl.ds(0, 3)]
         else:
             part = pl.ds(0 if dc < 0 else 4 * own * REACH - PACK, PACK)
             src = rows_out.at[0 if dr < 0 else 1, part]
@@ -454,6 +458,14 @@
         return pltpu.make_async_remote_copy(
             src_ref=src, dst_ref=dst, send_sem=near_send.at[k], recv_sem=near_recv.at[k],
             device_id=(my_row + dr, my_col + dc), device_id_type=MESH,
+        )
+
+    def side_copy(side):
+        return pltpu.make_async_remote_copy(
+            src_ref=near.at[3, (0, own - 1)[side], pl.ds(0, rows)],
+            dst_ref=sides_in.at[side, 3],
+            send_sem=near_send.at[len(OFFSETS) + side], recv_sem=near_recv.at[len(OFFSETS) + side],
+            device_id=(my_row, my_col + (-1, 1)[side]), device_id_type=MESH,
         )
 
     def window_copy(field, half, q):
@@ -465,21 +477,83 @@
             device_id=(peer, my_col), device_id_type=MESH,
         )
 
-    def send_window(field, early, late):
+    def part_copy(half, q, piece):
+        peer = lax.rem(my_row + q, row_peers)
+        start, size = ((SUB, rows - 2 * SUB), (0, SUB), (rows - SUB, SUB))[piece]
+        send, recv = (peer_send, peer_recv) if piece == 0 else (rim_send, rim_recv)
+        at = (1, half, q) if piece == 0 else (piece - 1, half, q)
+        return pltpu.make_async_remote_copy(
+            src_ref=shifted.at[1, peer + half, pl.ds(start, size)],
+            dst_ref=window.at[1, half, pl.ds(pl.multiple_of(my_row * rows + start, SUB), size)],
+            send_sem=send.at[at], recv_sem=recv.at[at],
+            device_id=(peer, my_col), device_id_type=MESH,
+        )
+
+    def place(field):
+        window[field, :, pl.ds(pl.multiple_of(my_row * rows, rows), rows)] = shifted[
+            field, pl.ds(my_row, 2)
+        ]
+
+    def each(target, act):
         for q in range(1, row_peers):
-            peer = lax.rem(my_row + q, row_peers)
             for half in (0, 1):
-                edge = peer == (0, row_peers - 1)[half]
-                if early and late:
-                    window_copy(field, half, q).start()
-                else:
-                    @pl.when(edge if late else jnp.logical_not(edge))
-                    def _(half=half, q=q):
-                        window_copy(field, half, q).start()
-        if late:
-            window[field, :, pl.ds(pl.multiple_of(my_row * rows, rows), rows)] = shifted[
-                field, pl.ds(my_row, 2)
-            ]
+                row = lax.rem(my_row + q, row_peers) if target else my_row
+                act(half, q, row == (0, row_peers - 1)[half])
+
+    def send_route(late):
+        def act(half, q, edge):
+            @pl.when(edge if late else jnp.logical_not(edge))
+            def _():
+                window_copy(0, half, q).start()
+
+        each(True, act)
+
+    def send_inner():
+        def act(half, q, edge):
+            @pl.when(jnp.logical_not(edge))
+            def _():
+                part_copy(half, q, 0).start()
+
+        each(True, act)
+
+    def send_rest():
+        def act(half, q, edge):
+            @pl.when(edge)
+            def _():
+                window_copy(1, half, q).start()
+
+            @pl.when(jnp.logical_not(edge))
+            def _():
+                part_copy(half, q, 1).start()
+                part_copy(half, q, 2).start()
+
+        each(True, act)
+
+    def receive_level():
+        def act(half, q, edge):
+            @pl.when(edge)
+            def _():
+                window_copy(1, half, q).wait_recv()
+
+            @pl.when(jnp.logical_not(edge))
+            def _():
+                for piece in range(3):
+                    part_copy(half, q, piece).wait_recv()
+
+        each(False, act)
+
+    def level_sent():
+        def act(half, q, edge):
+            @pl.when(edge)
+            def _():
+                window_copy(1, half, q).wait_send()
+
+            @pl.when(jnp.logical_not(edge))
+            def _():
+                for piece in range(3):
+                    part_copy(half, q, piece).wait_send()
+
+        each(True, act)
 
     def receive_window(field):
         for q in range(1, row_peers):
@@ -493,67 +567,29 @@
 
     order = (1, 3, 5, 7, 2, 6, 0, 4)
     pl.semaphore_wait(barrier, expected)
+    for side, dc in enumerate((-1, 1)):
+        @pl.when(exists(0, dc))
+        def _(side=side):
+            side_copy(side).start()
     for k in order:
         @pl.when(exists(*OFFSETS[k]))
         def _(k=k):
             near_copy(k).start()
     shift_tiles(0, route_tile, range(1, own))
-    send_window(0, True, False)
-
-    blank = pl.ds(rows + REACH, total - rows - 2 * REACH)
-    near[:, :, blank] = jnp.zeros((4, own + 2, total - rows - 2 * REACH, LANES), f32)
-
-    for k in order:
-        dr, dc = OFFSETS[k]
-        there = exists(-dr, -dc)
-
-        @pl.when(there)
-        def _(k=k):
-            near_copy(k).wait_recv()
-
-        @pl.when(jnp.logical_not(there))
-        def _(k=k):
-            dst = near_ends(k)[1]
-            dst[...] = jnp.zeros(dst.shape, f32)
-
-    below, above = pl.ds(rows, REACH), pl.ds(total - REACH, REACH)
-    for a in range(4):
-        for c in range(own):
-            at = pl.ds((c * 4 + a) * REACH, REACH)
-            near[a, c, below] = rows_in[1, at]
-            near[a, c, above] = rows_in[0, at]
-        for k in (1, 3, 5, 7):
-            dr, dc = OFFSETS[k]
-            start = 0 if dc < 0 else PACK - 4 * REACH
-            near[a, east if dc < 0 else west, below if dr < 0 else above] = corners_in[
-                k, pl.ds(start + a * REACH, REACH)
-            ]
-
-    shift_tiles(0, route_tile, (0, own))
-    send_window(0, False, True)
+    send_route(False)
+
+    near[:, pl.ds(0, own), pl.ds(rows, total - rows)] = jnp.zeros((4, own, total - rows, LANES), f32)
+    near[:, pl.ds(own, 2), pl.ds(0, total)] = jnp.zeros((4, 2, total, LANES), f32)
 
     def near_band(a, v):
         take = pl.ds(v, SUB, stride=thin)
         return jnp.concatenate([near[a, c, take, :] for c in range(own + 2)], axis=1)
-
-    for v in range(thin):
-        h[v] = near_band(0, v)
-        rain[v] = near_band(1, v)
-        coef[v] = near_band(2, v)
-        base[v] = near_band(3, v)
 
     def mask_rows(dst, count, up, here, down):
         for v in range(count):
             rows_near = {1: up(v), 0: here(v), -1: down(v)}
             for k, (di, dj) in enumerate(OFFSETS):
                 dst[k, v] = jnp.where(rows_near[di] == k + 1, f32(1.0), f32(0.0))
-
-    mask_rows(
-        near_masks, thin,
-        lambda v: base[v - 1] if v else pltpu.roll(base[thin - 1], 1, 0),
-        lambda v: base[v],
-        lambda v: base[v + 1] if v < thin - 1 else pltpu.roll(base[0], SUB - 1, 0),
-    )
 
     def sweep(field, mask, count, width, finish):
         start = field[0]
@@ -570,26 +606,94 @@
             )
             up, here = here, down
 
-    @pl.loop(0, SUBSTEPS)
-    def _(step):
+    def levels():
         for v in range(thin):
-            depth = h[v]
-            factor = coef[v] * jnp.exp(jnp.log(depth) * f32(2.0 / 3.0))
-            out = depth * (factor / (1.0 + factor))
-            share[v] = out
-            base[v] = depth + rain[v] - out
-
-        def finish(v, came):
-            h[v] = base[v] + came
-
-        sweep(share, near_masks, thin, wide, finish)
-
-    for v in range(thin):
-        value = h[v]
-        for c in range(own + 2):
-            plain[c, pl.ds(v, SUB, stride=thin), :] = value[:, c * LANES : (c + 1) * LANES]
-    shift_tiles(1, lambda c, tile: plain[c, tile], range(own + 1))
-    send_window(1, True, True)
+            h[v] = near_band(0, v)
+            rain[v] = near_band(1, v)
+            coef[v] = near_band(2, v)
+            base[v] = near_band(3, v)
+
+        mask_rows(
+            near_masks, thin,
+            lambda v: base[v - 1] if v else pltpu.roll(base[thin - 1], 1, 0),
+            lambda v: base[v],
+            lambda v: base[v + 1] if v < thin - 1 else pltpu.roll(base[0], SUB - 1, 0),
+        )
+
+        @pl.loop(0, SUBSTEPS)
+        def _(step):
+            for v in range(thin):
+                depth = h[v]
+                factor = coef[v] * jnp.exp(jnp.log(depth) * f32(2.0 / 3.0))
+                out = depth * (factor / (1.0 + factor))
+                share[v] = out
+                base[v] = depth + rain[v] - out
+
+            def finish(v, came):
+                h[v] = base[v] + came
+
+            sweep(share, near_masks, thin, wide, finish)
+
+        for v in range(thin):
+            value = h[v]
+            for c in range(own + 2):
+                plain[c, pl.ds(v, SUB, stride=thin), :] = value[:, c * LANES : (c + 1) * LANES]
+
+    def level_tile(c, tile):
+        return plain[c, tile]
+
+    levels()
+    shift_tiles(1, level_tile, range(1, own), inner)
+    send_inner()
+    for side, dc in enumerate((-1, 1)):
+        there = exists(0, -dc)
+
+        @pl.when(there)
+        def _(side=side):
+            side_copy(side).wait_recv()
+
+        @pl.when(jnp.logical_not(there))
+        def _(side=side):
+            sides_in[side, 3] = jnp.zeros((rows, LANES), f32)
+
+        near[3, own + side, pl.ds(0, rows)] = sides_in[side, 3]
+    shift_tiles(0, route_tile, (0, own))
+    send_route(True)
+    place(0)
+    for k in order:
+        dr, dc = OFFSETS[k]
+        there = exists(-dr, -dc)
+
+        @pl.when(there)
+        def _(k=k):
+            near_copy(k).wait_recv()
+
+        @pl.when(jnp.logical_not(there))
+        def _(k=k):
+            dst = near_ends(k)[1]
+            dst[...] = jnp.zeros(dst.shape, f32)
+
+    below, above = pl.ds(rows, REACH), pl.ds(total - REACH, REACH)
+    for a in range(4):
+        for c in range(own):
+            at = pl.ds((c * 4 + a) * REACH, REACH)
+            near[a, c, below] = rows_in[1, at]
+            near[a, c, above] = rows_in[0, at]
+        for k in (1, 3, 5, 7):
+            dr, dc = OFFSETS[k]
+            start = 0 if dc < 0 else PACK - 4 * REACH
+            near[a, east if dc < 0 else west, below if dr < 0 else above] = corners_in[
+                k, pl.ds(start + a * REACH, REACH)
+            ]
+
+    for side in (0, 1):
+        near[pl.ds(0, 3), own + side, pl.ds(0, rows)] = sides_in[side, pl.ds(0, 3)]
+
+    levels()
+    shift_tiles(1, level_tile, (0, own))
+    shift_tiles(1, level_tile, range(1, own), rim)
+    send_rest()
+    place(1)
     for c in range(own):
         out_ref[0, :, pl.ds(c * LANES, LANES)] = plain[c, pl.ds(0, rows)]
 
@@ -623,7 +727,7 @@
                     elif (di, b) == (-1, 0):
                         here = here & (along > 0)
                     masks[k, v, b] = jnp.where(here, f32(1.0), f32(0.0))
-    receive_window(1)
+    receive_level()
     lay(1)
 
     def pair(ref, v):
@@ -706,8 +810,12 @@
         @pl.when(exists(*OFFSETS[k]))
         def _(k=k):
             near_copy(k).wait_send()
+    for side, dc in enumerate((-1, 1)):
+        @pl.when(exists(0, dc))
+        def _(side=side):
+            side_copy(side).wait_send()
     window_sent(0)
-    window_sent(1)
+    level_sent()
     for q in range(1, row_peers):
         result_copy(q).wait_recv()
     for q in range(1, row_peers):
@@ -732,6 +840,7 @@
             pltpu.VMEM(tile, i32),
             pltpu.VMEM(tile, i32),
             pltpu.VMEM((4, own + 2, total + SUB, LANES), f32),
+            pltpu.VMEM((2, 4, rows, LANES), f32),
             pltpu.VMEM((2, 4 * own * REACH + SUB, LANES), f32),
             pltpu.VMEM((2, 4 * own * REACH + SUB, LANES), f32),
             pltpu.VMEM((len(OFFSETS), PACK + SUB, LANES), f32),
@@ -751,10 +860,12 @@
             pltpu.VMEM((2, 2 * LANES, LANES), f32),
             pltpu.VMEM((row_peers * rows, LANES), f32),
             pltpu.SemaphoreType.DMA((3 + 2 * own,)),
-            pltpu.SemaphoreType.DMA((len(OFFSETS),)),
-            pltpu.SemaphoreType.DMA((len(OFFSETS),)),
+            pltpu.SemaphoreType.DMA((len(OFFSETS) + 2,)),
+            pltpu.SemaphoreType.DMA((len(OFFSETS) + 2,)),
             pltpu.SemaphoreType.DMA((3, 2, row_peers)),
             pltpu.SemaphoreType.DMA((3, 2, row_peers)),
+            pltpu.SemaphoreType.DMA((2, 2, row_peers)),
+            pltpu.SemaphoreType.DMA((2, 2, row_peers)),
         ]
         + [
             pltpu.VMEM((len(OFFSETS), count, 2, SUB, LANES), f32)

time: 28.6 us -> 28.3 us (0.990)
  Pallas kernels: 27.1 us -> 26.8 us
    pallas_call x1, Pallas kernels: 27.1 us -> 26.8 us  [on_device(): both = strip_call(row_peers, col_peers, rows, cols)(*args)]
where the time goes in v5:
time: 28.3 us; the launch traced here: 28.2 us
  Pallas kernels  26.8 us (95%)
  local copies, waits for them, and re-layouts  0.72 us (3%)
  between operations  0.64 us (2%)
    pallas_call x1, Pallas kernels, on_device(): both = strip_call(row_peers, col_peers, rows, cols)(*args)  26.8 us
    squeeze x1, local copies, waits for them, and re-layouts, on_device(): return (both[0], both[1])  0.72 us

profile of v5, /device:TPU:0, one launch (start us, length us, event | category | flops | bytes accessed | tf_op | source)
XLA Modules:
  0.0 28.2 jit_solution(16643838055438192099)
XLA Ops:
  0.6 26.8 %shard_map.68 = f32[2,64,512]{2,1,0:T(8,128)S(1)} custom-call(f32[64,512]{1,0:T(8,128)} %depth_hbm.1, f32[64,512]{1,0:T(8,128)} %rain_hbm.1, f32[64,512]{1,0:T(8,128)} %conv_hbm.1, s32[64,512]{1,0:T(8,128)} %dir_hbm.1, s32[64,512]{1,0:T(8,128)} %outlet_hbm.1), custom_call_target="tpu_custom_call" | custom-call | tf_op jit(solution)/shard_map/pallas_call | solution.py:900
  27.5 0.7 %slice_bitcast_fusion = (f32[64,512]{1,0:T(8,128)}, f32[64,512]{1,0:T(8,128)}) fusion(f32[2,64,512]{2,1,0:T(8,128)S(1)} %shard_map.68), kind=kLoop, calls=%fused_computation | loop fusion | bytes 524288 | tf_op jit(solution)/shard_map/squeeze | solution.py:901

commit v6 on v5

--- a/solution.py
+++ b/solution.py
@@ -19,7 +19,7 @@
 HALF = LANES // 2
 REACH = 3
 PACK = 2 * SUB
-STAGES = (24, 20, 20)
+STAGES = (16, 16, 16, 16)
 VMEM_BYTES = 40 * 1024 * 1024
 MESH = pl.DeviceIdType.MESH
 
@@ -365,6 +365,19 @@
         r, c = my_row + dr, my_col + dc
         return (r >= 0) & (r < row_peers) & (c >= 0) & (c < col_peers)
 
+    loads = [
+        pltpu.make_async_copy(src, dst, load_sem.at[i])
+        for i, (src, dst) in enumerate(
+            [(conv_hbm, conv_ref), (dir_hbm, dir_ref), (outlet_hbm, outlet_ref)]
+            + [
+                (src.at[:, pl.ds(c * LANES, LANES)], near.at[a, c, pl.ds(0, rows)])
+                for a, src in enumerate((depth_hbm, rain_hbm))
+                for c in range(own)
+            ]
+        )
+    ]
+    for load in loads:
+        load.start()
     barrier = pltpu.get_barrier_semaphore()
 
     def greet(row, col):
@@ -384,19 +397,6 @@
         def _(q=q):
             greet(q, my_col)
 
-    loads = [
-        pltpu.make_async_copy(src, dst, load_sem.at[i])
-        for i, (src, dst) in enumerate(
-            [(conv_hbm, conv_ref), (dir_hbm, dir_ref), (outlet_hbm, outlet_ref)]
-            + [
-                (src.at[:, pl.ds(c * LANES, LANES)], near.at[a, c, pl.ds(0, rows)])
-                for a, src in enumerate((depth_hbm, rain_hbm))
-                for c in range(own)
-            ]
-        )
-    ]
-    for load in loads:
-        load.start()
     for load in loads:
         load.wait()
 
@@ -757,10 +757,17 @@
 
         @pl.loop(0, passes // 2)
         def _(index):
-            left, here = turn(pair(acc, count - 1), 1), pair(acc, 0)
+            last = count - 1
+            first = pair(acc, 0)
+            edge = gather(
+                fetch(last), pair(level, last), pair(acc, last - 1), pair(acc, last),
+                turn(first, SUB - 1),
+            )
+            put(hold, 2, edge)
+            left, here = turn(pair(acc, last), 1), first
             older = newer = held = seed = None
-            for v in range(count):
-                right = pair(acc, v + 1) if v < count - 1 else turn(pair(acc, 0), SUB - 1)
+            for v in range(last):
+                right = pair(acc, v + 1)
                 fresh, start = fetch(v), pair(level, v)
                 value = gather(fresh, start, left, here, right)
                 if v < 2:
@@ -770,10 +777,15 @@
                 older, newer = newer, value
                 held, seed = fresh, start
                 left, here = here, right
-            put(acc, count - 1, gather(held, seed, older, newer, turn(pair(hold, 0), SUB - 1)))
+            edge = pair(hold, 2)
+            put(acc, last - 1, gather(held, seed, older, newer, edge))
+            put(
+                acc, last,
+                gather(fetch(last), pair(level, last), newer, edge, turn(pair(hold, 0), SUB - 1)),
+            )
             put(
                 acc, 0,
-                gather(fetch(0), pair(level, 0), turn(newer, 1), pair(hold, 0), pair(hold, 1)),
+                gather(fetch(0), pair(level, 0), turn(edge, 1), pair(hold, 0), pair(hold, 1)),
             )
 
     source = tall
@@ -855,7 +867,7 @@
             pltpu.VMEM((2, 2, row_peers * rows, LANES), f32),
             pltpu.VMEM(field, f32),
             pltpu.VMEM(field, f32),
-            pltpu.VMEM((2, 2, SUB, LANES), f32),
+            pltpu.VMEM((3, 2, SUB, LANES), f32),
             pltpu.VMEM((2, 2 * LANES, LANES), f32),
             pltpu.VMEM((2, 2 * LANES, LANES), f32),
             pltpu.VMEM((row_peers * rows, LANES), f32),

time: 28.3 us -> 28.1 us (level)
  no operation moved by 1% of the time
where the time goes in v6:
time: 28.1 us; the launch traced here: 28 us
  Pallas kernels  26.6 us (95%)
  local copies, waits for them, and re-layouts  0.72 us (3%)
  between operations  0.64 us (2%)
    pallas_call x1, Pallas kernels, on_device(): both = strip_call(row_peers, col_peers, rows, cols)(*args)  26.6 us
    squeeze x1, local copies, waits for them, and re-layouts, on_device(): return (both[0], both[1])  0.72 us

profile of v6, /device:TPU:0, one launch (start us, length us, event | category | flops | bytes accessed | tf_op | source)
XLA Modules:
  0.0 28.0 jit_solution(586621566958629230)
XLA Ops:
  0.6 26.6 %shard_map.68 = f32[2,64,512]{2,1,0:T(8,128)S(1)} custom-call(f32[64,512]{1,0:T(8,128)} %depth_hbm.1, f32[64,512]{1,0:T(8,128)} %rain_hbm.1, f32[64,512]{1,0:T(8,128)} %conv_hbm.1, s32[64,512]{1,0:T(8,128)} %dir_hbm.1, s32[64,512]{1,0:T(8,128)} %outlet_hbm.1), custom_call_target="tpu_custom_call" | custom-call | tf_op jit(solution)/shard_map/pallas_call | solution.py:912
  27.3 0.7 %slice_bitcast_fusion = (f32[64,512]{1,0:T(8,128)}, f32[64,512]{1,0:T(8,128)}) fusion(f32[2,64,512]{2,1,0:T(8,128)S(1)} %shard_map.68), kind=kLoop, calls=%fused_computation | loop fusion | bytes 524288 | tf_op jit(solution)/shard_map/squeeze | solution.py:913
